TPU v7x, 256 devices: a whole 4x4x8 slice. The times are simulated.
256 devices in a mesh: occ: 8 (over x, z_hi), vir: 8 (over z_lo, core), aux: 4 (over y).
Axes of the slice: x: 4, y: 4, z: 8 (z_hi: 2, z_lo: 4; z = z_hi * 4 + z_lo), core: 2. Of those that a mesh axis runs over, the one named last changes fastest.
Arguments:
- amplitudes: bfloat16 [64, 1024, 1024], P('occ', 'vir'), may hold values from -6 to 6
- pair_mask: int32 [64, 8, 8], P('occ', 'vir'), may hold values 0 or 1
- left_factor: bfloat16 [32, 1024, 4096], P(None, 'vir', 'aux'), may hold values from -0.0390625 to 0.0390625
- left_mask: int32 [8, 32], P('vir', 'aux'), may hold values 0 or 1
- right_factor: bfloat16 [1024, 4, 4096], P(('occ', 'vir'), None, 'aux'), may hold values from -0.0390625 to 0.0390625
- right_mask: int32 [8, 32], P(None, 'aux'), may hold values 0 or 1
- residual_in: float32 [64, 4, 32], P('occ'), may hold values from -6 to 6
Outputs:
- updated: float32 [64, 4, 32], P('occ')
All inputs are finite; a program needn't handle non-finite values. No bound on the sum of `pair_mask` or of `left_mask` or of `right_mask` on one device may be relied on, other than what follows from the above.
Results may differ from a plain program's by a relative error of at most 0.0003.
Values may be sent and summed in bfloat16 or wider, within the bound.
A program may use at most 128 MiB of HBM per device.

v0:
```python
import jax
import jax.numpy as jnp
from jax import lax
from jax.sharding import PartitionSpec as P

TILE = 128


def joined_along(tiles, dim):
    lengths = list(tiles.shape[1:])
    lengths[dim] *= tiles.shape[0]
    return jnp.moveaxis(tiles, 0, dim).reshape(lengths)


def from_everyone(value, axis):
    copies = jnp.broadcast_to(value, (lax.axis_size(axis), *value.shape))
    return lax.all_to_all(copies, axis, split_axis=0, concat_axis=0, tiled=True)


def gathered_copies(value, axis, dim):
    return joined_along(from_everyone(value, axis), dim)


def cut_along(value, dim, devices):
    before, after = (value.shape[:dim], value.shape[dim + 1 :])
    return jnp.moveaxis(value.reshape(*before, devices, -1, *after), dim, 0)


def sent_and_summed(value, axis, dim):
    tiles = cut_along(value, dim, lax.axis_size(axis))
    arrived = lax.all_to_all(tiles, axis, split_axis=0, concat_axis=0, tiled=True)
    return arrived.sum(axis=0)


def of_everyone(value, axis):
    everything = from_everyone(value, axis)
    return jnp.sum(everything, axis=0)


def expand_tiles(mask, width):
    return jnp.repeat(jnp.repeat(mask, width, axis=-2), width, axis=-1)


def local(amplitudes, pair_mask, left_factor, left_mask, right_factor, right_mask, residual_in):
    pairs_here, cols_here, virt_all = amplitudes.shape
    rows_here, block_b, aux_here = right_factor.shape
    block_a = left_factor.shape[0]
    tau = amplitudes * expand_tiles(pair_mask, TILE).astype(jnp.bfloat16)
    left = left_factor * expand_tiles(left_mask, TILE).astype(jnp.bfloat16)[None, :, :]
    tiles_all = right_mask.shape[0]
    aux_mask = jnp.repeat(right_mask, TILE, axis=1).astype(jnp.float32)
    row_start = lax.axis_index(("occ", "vir")) * rows_here
    row_tiles = (row_start + jnp.arange(rows_here, dtype=jnp.int32)) // TILE
    onehot = (row_tiles[:, None] == jnp.arange(tiles_all, dtype=jnp.int32)[None, :]).astype(
        jnp.float32
    )
    row_mask = jnp.dot(onehot, aux_mask, preferred_element_type=jnp.float32)
    right = right_factor * row_mask.astype(jnp.bfloat16)[:, None, :]
    tau_moved = lax.all_to_all(tau, "occ", split_axis=2, concat_axis=0, tiled=True)
    right_near = gathered_copies(right, "vir", 0)
    rows_near = right_near.shape[0]
    couple = jnp.einsum("acq,dbq->cdba", left, right_near, preferred_element_type=jnp.float32)
    couple_flat = couple.reshape(cols_here * rows_near, block_b * block_a)
    all_pairs = tau_moved.shape[0]
    tau_wide = tau_moved.reshape(all_pairs, cols_here * rows_near).astype(jnp.float32)
    every_pair = jnp.dot(
        tau_wide, couple_flat, precision=lax.Precision.HIGHEST, preferred_element_type=jnp.float32
    )
    every_pair = every_pair.reshape(all_pairs, block_b, block_a)
    partial_sum = sent_and_summed(every_pair, "occ", 0)
    total = of_everyone(partial_sum, ("vir", "aux"))
    return residual_in + total


def solution(mesh):
    return jax.shard_map(
        local,
        mesh=mesh,
        in_specs=(
            P("occ", "vir", None),
            P("occ", "vir", None),
            P(None, "vir", "aux"),
            P("vir", "aux"),
            P(("occ", "vir"), None, "aux"),
            P(None, "aux"),
            P("occ", None, None),
        ),
        out_specs=P("occ", None, None),
        check_vma=False,
    )
```

profile of v0, /device:TPU:1, one launch (start us, length us, event | category | flops | bytes accessed | tf_op | source)
XLA Modules:
  0.0 145.1 jit_solution(8518812949693570374)
XLA Ops:
  0.0 0.7 convert_element_type.38
  0.7 0.1 broadcast_bitcast_fusion
  0.8 0.2 convolution_convert_fusion
  1.0 1.0 broadcast_multiply_fusion.1
  2.0 1.1 broadcast_in_dim.26
  3.2 7.4 %all-to-all-start.1 = ((bf16[8,16,4,1024]{3,1,2,0:T(8,128)(2,1)}), bf16[8,16,4,1024]{3,1,2,0:T(8,128)(2,1)S(1)}, u32[]{:S(2)}, u32[]{:S(2)}) async-start(bf16[8,16,4,1024]{3,1,2,0:T(8,128)(2,1)} %broadcast_in_dim.26), calls=%async_computation.1 | async-start | bytes 2097152 | tf_op jit(solution)/shard_map/all_to_all | solution.py:17
  10.5 3.4 %copy.27 = bf16[8,128,1024]{1,0,2:T(8,128)(2,1)S(1)} copy(bf16[8,128,1024]{2,1,0:T(8,128)(2,1)} %param.7) | data formatting | bytes 4194304 | tf_op args[0]
  13.9 0.7 convert_bitcast_fusion
  14.6 0.1 copy.26
  14.7 2.3 %broadcast_multiply_fusion = bf16[8,128,1024]{1,0,2:T(8,128)(2,1)} fusion(bf16[8,128,1024]{1,0,2:T(8,128)(2,1)S(1)} %copy.27, bf16[8,1024]{0,1:T(8,128)(2,1)S(1)} %bitcast.62), kind=kLoop, calls=%fused_computation.9 | loop fusion | flops 1048576 | bytes 4210688 | tf_op jit(solution)/shard_map/mul | solution.py:48
  17.0 19.1 %all-to-all-done.1 = bf16[8,16,4,1024]{3,1,2,0:T(8,128)(2,1)S(1)} async-done(((bf16[8,16,4,1024]{3,1,2,0:T(8,128)(2,1)}), bf16[8,16,4,1024]{3,1,2,0:T(8,128)(2,1)S(1)}, u32[]{:S(2)}, u32[]{:S(2)}) %all-to-all-start.1) | async-done | bytes 1048608 | tf_op jit(solution)/shard_map/all_to_all | solution.py:17
  36.1 8.2 %all-to-all-start = ((bf16[8,128,1024]{1,0,2:T(8,128)(2,1)}), bf16[8,128,1024]{1,0,2:T(8,128)(2,1)S(1)}, u32[]{:S(2)}, u32[]{:S(2)}) async-start(bf16[8,128,1024]{1,0,2:T(8,128)(2,1)} %broadcast_multiply_fusion), calls=%async_computation | async-start | bytes 4194304 | tf_op jit(solution)/shard_map/all_to_all | solution.py:59
  44.4 0.1 broadcast_bitcast_fusion.1
  44.5 0.1 copy.30
  44.5 9.0 %fusion.4 = f32[128,128,4,32]{0,1,3,2:T(8,128)} fusion(bf16[128,4,1024,1]{2,0,3,1:T(8,128)(2,1)S(1)} %bitcast.63, bf16[32,128,1024]{2,1,0:T(8,128)(2,1)} %param.9, bf16[1024]{0:T(1024)(128)(2,1)S(1)} %broadcast_bitcast_fusion.1), kind=kOutput, calls=%fused_computation.5 | convolution fusion | flops 4311744512 | bytes 17827840 | tf_op jit(solution)/shard_map/acq,dbq->cdba/dot_general | solution.py:62
  53.6 8.9 %copy.31 = f32[128,128,4,32]{1,0,3,2:T(8,128)} copy(f32[128,128,4,32]{0,1,3,2:T(8,128)} %fusion.4) | data formatting | bytes 16777216 | tf_op jit(solution)/shard_map/acq,dbq->cdba/transpose | solution.py:62
  62.5 13.1 %copy.44 = f32[16,8,128,128]{3,1,2,0:T(8,128)} copy(f32[16,8,128,128]{3,2,1,0:T(8,128)} %bitcast.59) | data formatting | bytes 16777216
  75.6 18.8 %all-to-all-done = bf16[8,128,1024]{1,0,2:T(8,128)(2,1)S(1)} async-done(((bf16[8,128,1024]{1,0,2:T(8,128)(2,1)}), bf16[8,128,1024]{1,0,2:T(8,128)(2,1)S(1)}, u32[]{:S(2)}, u32[]{:S(2)}) %all-to-all-start) | async-done | bytes 2097184 | tf_op jit(solution)/shard_map/all_to_all | solution.py:59
  94.4 3.2 %copy.28 = bf16[8,128,8,128]{3,0,1,2:T(8,128)(2,1)} copy(bf16[8,128,8,128]{1,0,3,2:T(8,128)(2,1)S(1)} %bitcast.61) | data formatting | bytes 4194304 | tf_op jit(solution)/shard_map/all_to_all | solution.py:59
  97.6 13.2 %fusion.12 = f32[8,4,8,32]{3,2,1,0:T(8,128)S(1)} fusion(f32[4,32,16384,1]{2,1,0,3:T(8,128)} %bitcast.60, bf16[8,128,8,128]{3,0,1,2:T(8,128)(2,1)} %copy.28), kind=kOutput, calls=%fused_computation.24 | convolution fusion | flops 1610612736 | bytes 10518528 | tf_op jit(solution)/shard_map/dot_general | solution.py:66
  110.8 0.1 reshape.52
  110.9 13.3 %all_to_all.30 = f32[8,1,1024]{2,1,0:T(1,128)S(1)} all-to-all(f32[8,1,1024]{2,1,0:T(1,128)S(1)} %reshape.52), channel_id=1, replica_groups=mesh['occ'=8,'vir'=8,'aux'=4] {'occ'}, dimensions={0} | all-to-all | bytes 65536 | tf_op jit(solution)/shard_map/all_to_all | solution.py:31
  124.2 0.5 broadcast.60
  124.7 0.7 reduce
  125.5 0.1 reshape.53
  125.6 0.1 broadcast_bitcast_fusion.2
  125.6 0.3 reshape.54
  125.9 17.4 %all_to_all.31 = f32[32,1,1024]{2,1,0:T(1,128)S(1)} all-to-all(f32[32,1,1024]{2,1,0:T(1,128)S(1)} %reshape.54), channel_id=1, replica_groups=mesh['occ'=8,'vir'=8,'aux'=4] {'vir','aux'}, dimensions={0} | all-to-all | bytes 262144 | tf_op jit(solution)/shard_map/all_to_all | solution.py:17
  143.3 1.0 reduce.1
  144.3 0.2 reshape.55
  144.4 0.1 bitcast_reduce_fusion
  144.5 0.6 copy.33
  (10 shorter events, 0.1 us)
Async XLA Ops:
  2.0 42.4 %copy-start.1 = (s32[1,8]{1,0:T(1,128)S(1)}, s32[1,8]{1,0:T(1,128)}, u32[]{:S(2)}) copy-start(s32[1,8]{1,0:T(1,128)} %param.10) | copy-start | bytes 100
  3.2 33.0 %all-to-all-start.1 = ((bf16[8,16,4,1024]{3,1,2,0:T(8,128)(2,1)}), bf16[8,16,4,1024]{3,1,2,0:T(8,128)(2,1)S(1)}, u32[]{:S(2)}, u32[]{:S(2)}) async-start(bf16[8,16,4,1024]{3,1,2,0:T(8,128)(2,1)} %broadcast_in_dim.26), calls=%async_computation.1 | async-start | bytes 2097152 | tf_op jit(solution)/shard_map/all_to_all | solution.py:17
  36.1 58.2 %all-to-all-start = ((bf16[8,128,1024]{1,0,2:T(8,128)(2,1)}), bf16[8,128,1024]{1,0,2:T(8,128)(2,1)S(1)}, u32[]{:S(2)}, u32[]{:S(2)}) async-start(bf16[8,128,1024]{1,0,2:T(8,128)(2,1)} %broadcast_multiply_fusion), calls=%async_computation | async-start | bytes 4194304 | tf_op jit(solution)/shard_map/all_to_all | solution.py:59
  97.6 46.9 %copy-start = (f32[8,4,32]{2,1,0:T(4,128)S(1)}, f32[8,4,32]{2,1,0:T(4,128)}, u32[]{:S(2)}) copy-start(f32[8,4,32]{2,1,0:T(4,128)} %param.13) | copy-start | bytes 12292
where the time goes:
time: 146 us; the launch traced here: 145 us
  waiting for transfers between devices  37.9 us (26%)
  local copies, waits for them, and re-layouts  32 us (22%)
  blocking collectives  30.7 us (21%)
  matrix products  22.4 us (15%)
  starting transfers between devices  15.6 us (11%)
  other arithmetic  6.41 us (4%)
    all_to_all x1, waiting for transfers between devices, from_everyone(): return lax.all_to_all(copies, axis, split_axis=0, concat_axis=0, tiled=True)  19.1 us
    all_to_all x1, waiting for transfers between devices, local(): lax.all_to_all(tau, 'occ', split_axis=2, concat_axis=0, tiled=True)  18.8 us
    all_to_all x1, blocking collectives, from_everyone(): return lax.all_to_all(copies, axis, split_axis=0, concat_axis=0, tiled=True)  17.4 us
    unnamed x12, local copies, waits for them, and re-layouts  17.3 us
    all_to_all x1, blocking collectives, sent_and_summed(): lax.all_to_all(tiles, axis, split_axis=0, concat_axis=0, tiled=True)  13.3 us
    dot_general x1, matrix products, local(): jnp.dot(tau_wide, couple_flat, precision=lax.Precision.HIGHEST, preferred...  13.2 us
    dot_general x1, matrix products, local(): jnp.einsum('acq,dbq->cdba', left, right_near, preferred_element_type=jnp....  9.01 us
    transpose x1, local copies, waits for them, and re-layouts, local(): jnp.einsum('acq,dbq->cdba', left, right_near, preferred_element_type=jnp....  8.93 us
  transfers between devices with their start and end apart: 2, of which 2 were waited for; matrix products, arithmetic and copies ran while one was open for 26% of the time, Pallas kernels for 0%

commit v1 on v0

v1 whole, which is shorter than its diff:
```python
import functools

import jax
import jax.numpy as jnp
from jax import lax
from jax.experimental import pallas as pl
from jax.experimental.pallas import tpu as pltpu
from jax.sharding import PartitionSpec as P

TILE = 128
NX, NY, NZ = 4, 4, 8
BF, F32 = jnp.bfloat16, jnp.float32
MESH = pl.DeviceIdType.MESH
NT = (((1,), (1,)), ((), ()))


def device(x, y, z, core):
    return {"occ": 2 * x + z // 4, "vir": 2 * (z % 4) + core, "aux": y}


def kernel(
    amp, pmask, left_h, right_h, qmask, out_ref,
    left, rows, rmask, tau, pm, tw, chi, clo, grid_acc, part, got_xy, got_z, mine_z,
    local_sem, ring_send, ring_recv, pair_send, pair_recv,
    tx_send, tx_recv, ty_send, ty_recv, pm_send, pm_recv,
    xy_send, xy_recv, z_send, z_recv,
):
    occ, vir, y = lax.axis_index("occ"), lax.axis_index("vir"), lax.axis_index("aux")
    x, z, core = occ // 2, (occ % 2) * 4 + vir // 2, vir % 2
    here = pl.multiple_of(core * 16, 16)

    local = []
    for block in range(4):
        local.append(pltpu.make_async_copy(
            left_h.at[pl.ds(block * 8, 8)], left.at[pl.ds(block * 8, 8)], local_sem.at[block]))
    own_right = pltpu.make_async_copy(
        right_h, rows.at[:, pl.ds(32 + here, 16), :], local_sem.at[4])
    own_tau = pltpu.make_async_copy(
        amp.at[:, :, pl.ds(pl.multiple_of(x * 256, 256), 256)], tau.at[0], local_sem.at[5])
    own_right.start()
    for copy in local:
        copy.start()
    own_tau.start()
    pm[0] = pmask[x]

    barrier = pltpu.get_barrier_semaphore()
    count = 0
    for dx in range(NX):
        for dy in range(NY):
            if dx or dy:
                pl.semaphore_signal(
                    barrier, inc=1, device_id=device((x + dx) % NX, (y + dy) % NY, z, core),
                    device_id_type=MESH)
                count += 1
    for dz in (1, NZ - 1):
        pl.semaphore_signal(
            barrier, inc=1, device_id=device(x, y, (z + dz) % NZ, core), device_id_type=MESH)
        count += 1
    for dv in range(1, 8):
        pl.semaphore_signal(
            barrier, inc=1, device_id={"occ": occ, "vir": (vir + dv) % 8, "aux": y},
            device_id_type=MESH)
        count += 1
    pl.semaphore_wait(barrier, count)

    sent = []

    def ring(way, step, piece):
        src_i, dst_i = ((1 - step) % 8, (-step) % 8) if way == 0 else (1 + step, step + 2)
        to = (z + 1) % NZ if way == 0 else (z + NZ - 1) % NZ
        return pltpu.make_async_remote_copy(
            src_ref=rows.at[pl.ds(2 * piece, 2), pl.ds(src_i * 32 + here, 16), :],
            dst_ref=rows.at[pl.ds(2 * piece, 2), pl.ds(dst_i * 32 + here, 16), :],
            send_sem=ring_send.at[way, step, piece], recv_sem=ring_recv.at[way, step, piece],
            device_id=device(x, y, to, core), device_id_type=MESH)

    def pair(i):
        return pltpu.make_async_remote_copy(
            src_ref=rows.at[:, pl.ds(i * 32 + here, 16), :],
            dst_ref=rows.at[:, pl.ds(i * 32 + here, 16), :],
            send_sem=pair_send.at[i], recv_sem=pair_recv.at[i],
            device_id=device(x, y, z, 1 - core), device_id_type=MESH)

    def go(copy):
        copy.start()
        sent.append(copy)

    def tau_x(dx, first, size, sem):
        to = (x + dx) % NX
        return pltpu.make_async_remote_copy(
            src_ref=amp.at[pl.ds(first, size), :, pl.ds(pl.multiple_of(to * 256, 256), 256)],
            dst_ref=tau.at[(-dx) % 4, pl.ds(first, size)],
            send_sem=tx_send.at[sem], recv_sem=tx_recv.at[sem],
            device_id=device(to, y, z, core), device_id_type=MESH)

    def tau_y(slot, first, size, dy):
        return pltpu.make_async_remote_copy(
            src_ref=tau.at[slot, pl.ds(first, size)], dst_ref=tau.at[slot, pl.ds(first, size)],
            send_sem=ty_send.at[slot, dy], recv_sem=ty_recv.at[slot, dy],
            device_id=device(x, (y + dy) % NY, z, core), device_id_type=MESH)

    def mask_x(dx):
        to = (x + dx) % NX
        return pltpu.make_async_remote_copy(
            src_ref=pmask.at[to], dst_ref=pm.at[(-dx) % 4],
            send_sem=pm_send.at[dx], recv_sem=pm_recv.at[dx],
            device_id=device(to, y, z, core), device_id_type=MESH)

    split = {1: (4 + y, 1), 2: (2 * y, 2), 3: (4 + y, 1)}
    own_right.wait()
    for piece in range(2):
        for way in range(2):
            go(ring(way, 0, piece))
    go(pair(1))
    x_split = {dx: tau_x(dx, *split[dx], dx) for dx in (2, 1, 3)}
    x_whole = {dx: tau_x(dx, 0, 4, 3 + dx) for dx in (1, 3)}
    masks = {dx: mask_x(dx) for dx in (1, 2, 3)}
    for copy in x_split.values():
        go(copy)
    for copy in masks.values():
        go(copy)
    for copy in x_whole.values():
        go(copy)

    def forward(step, nexts):
        for piece in range(2):
            for way in range(2):
                if (way, piece) not in RECEIVED[step]:
                    continue
                ring(way, step, piece).wait_recv()
                if (way, piece) in nexts:
                    go(ring(way, step + 1, piece))

    both = [(0, 0), (0, 1), (1, 0), (1, 1)]
    RECEIVED = {0: both, 1: both, 2: both, 3: [(0, 0), (1, 1)]}

    forward(0, both)
    go(pair(0))
    go(pair(2))
    y_copies = {}
    for dx in (2, 1, 3):
        x_split[dx].wait_recv()
        slot = (-dx) % 4
        for dy in (2, 1, 3):
            y_copies[slot, dy] = tau_y(slot, *split[dx], dy)
            go(y_copies[slot, dy])
    forward(1, both)
    go(pair(3))
    go(pair(7))

    def mask_rows(half):
        for i in range(4 * half, 4 * half + 4):
            pair(i).wait_recv()
        for i in range(4 * half, 4 * half + 4):
            tile = ((z + i + 7) % NZ) // 4
            row = qmask[pl.ds(tile, 1), :].astype(BF)
            for b in range(4):
                rmask[b * 128 + (i % 4) * 32: b * 128 + (i % 4) * 32 + 32, :] = (
                    rows[b, i * 32: i * 32 + 32, :] * row)

    def couple(half, block):
        lhs = left[block * 8: block * 8 + 8].reshape(8 * 128, 1024)
        prod = lax.dot_general(lhs, rmask[...], NT, preferred_element_type=F32)
        for g in range(16):
            blk = jnp.concatenate(
                [prod[a * 128 + g * 8: a * 128 + g * 8 + 8, :] for a in range(8)], axis=0)
            hi = blk.astype(BF)
            lo = (blk - hi.astype(F32)).astype(BF)
            for b in range(4):
                first = (b * 32 + block * 8) * 8
                chi[g, first: first + 64, half * 128: half * 128 + 128] = hi[:, b * 128: b * 128 + 128]
                clo[g, first: first + 64, half * 128: half * 128 + 128] = lo[:, b * 128: b * 128 + 128]

    for copy in local:
        copy.wait()
    mask_rows(0)
    couple(0, 0)
    couple(0, 1)
    forward(2, [(0, 0), (1, 1)])
    go(pair(6))
    go(pair(4))
    couple(0, 2)
    forward(3, [])
    go(pair(5))
    couple(0, 3)

    own_tau.wait()
    for dx in (1, 3):
        x_whole[dx].wait_recv()
    for dx in (1, 2, 3):
        masks[dx].wait_recv()
    for slot in (2, 3, 1):
        for dy in (1, 2, 3):
            y_copies[slot, dy].wait_recv()
    shift = ((9 - z) % 8) * 32

    def turn(step, _):
        slot, p = step // 4, (step % 4) * 2
        parts = []
        for k in range(2):
            block = tau[slot, p + k].astype(F32) * pm[slot, pl.ds(p + k, 1), :]
            parts.append(pltpu.roll(block, shift, 1))
        for g in range(16):
            pack = jnp.concatenate([v[g * 8: g * 8 + 8, :] for v in parts], axis=0)
            tw[g, pl.ds(pl.multiple_of(step * 16, 16), 16), :] = pack.astype(BF)
        return 0

    lax.fori_loop(0, 16, turn, 0)

    mask_rows(1)
    for block in range(4):
        couple(1, block)

    grid_acc[...] = jnp.zeros_like(grid_acc)

    def contract(step, _):
        total = grid_acc[...]
        for k in range(4):
            g = step * 4 + k
            total = total + lax.dot_general(chi[g], tw[g], NT, preferred_element_type=F32)
            total = total + lax.dot_general(clo[g], tw[g], NT, preferred_element_type=F32)
        grid_acc[...] = total
        return 0

    lax.fori_loop(0, 4, contract, 0)

    acc = grid_acc[...].reshape(128, 8, 256)
    same = (lax.broadcasted_iota(jnp.int32, (128, 8, 256), 2) % 8
            == lax.broadcasted_iota(jnp.int32, (128, 8, 256), 1))
    diag = jnp.where(same, acc, 0.0).sum(axis=1)
    pick = (lax.broadcasted_iota(jnp.int32, (32, 256), 1) // 8
            == lax.broadcasted_iota(jnp.int32, (32, 256), 0)).astype(F32).astype(BF)
    ladder = jnp.zeros((32, 128), F32)
    rest = diag
    for _ in range(3):
        top = rest.astype(BF)
        rest = rest - top.astype(F32)
        ladder = ladder + lax.dot_general(pick, top, NT, preferred_element_type=F32)
    part[...] = ladder.reshape(4, 8, 128)

    index = x * 4 + y
    got_xy[index] = part[0]

    def to_xy(dx, dy):
        return pltpu.make_async_remote_copy(
            src_ref=part.at[dx], dst_ref=got_xy.at[index],
            send_sem=xy_send.at[dx * 4 + dy], recv_sem=xy_recv.at[dx * 4 + dy],
            device_id=device((x + dx) % NX, (y + dy) % NY, z, core), device_id_type=MESH)

    pairs = [(dx, dy) for dx in range(4) for dy in range(4) if dx or dy]
    xy = [to_xy(dx, dy) for dx, dy in sorted(pairs, key=lambda d: -(d[0] == 2) - (d[1] == 2))]
    for copy in xy:
        go(copy)
    for copy in xy:
        copy.wait_recv()
    total = got_xy[0]
    for k in range(1, 16):
        total = total + got_xy[k]
    mine_z[...] = total
    got_z[vir] = total

    def to_z(dv):
        return pltpu.make_async_remote_copy(
            src_ref=mine_z, dst_ref=got_z.at[vir],
            send_sem=z_send.at[dv], recv_sem=z_recv.at[dv],
            device_id={"occ": occ, "vir": (vir + dv) % 8, "aux": y}, device_id_type=MESH)

    zs = [to_z(dv) for dv in range(1, 8)]
    for copy in zs:
        go(copy)
    for copy in zs:
        copy.wait_recv()
    total = got_z[0]
    for k in range(1, 8):
        total = total + got_z[k]
    out_ref[...] = total
    for copy in sent:
        copy.wait_send()


def local(amplitudes, pair_mask, left_factor, left_mask, right_factor, right_mask, residual_in):
    x = lax.axis_index("occ") // 2
    pmask = jnp.repeat(
        pair_mask.reshape(8, 4, 2).transpose(1, 0, 2).astype(F32), TILE, axis=2)
    tiles = lax.dynamic_slice_in_dim(right_mask, 2 * x, 2, axis=0) * left_mask
    qmask = jnp.repeat(tiles.astype(F32), TILE, axis=1)
    right_t = right_factor.transpose(1, 0, 2)
    dma = pltpu.SemaphoreType.DMA
    vmem = pltpu.VMEM
    any_spec = pl.BlockSpec(memory_space=pl.ANY)
    vmem_spec = pl.BlockSpec(memory_space=pltpu.VMEM)
    ladder = pl.pallas_call(
        kernel,
        out_shape=jax.ShapeDtypeStruct((8, 128), F32),
        in_specs=[any_spec, vmem_spec, any_spec, any_spec, vmem_spec],
        out_specs=vmem_spec,
        scratch_shapes=[
            vmem((32, 128, 1024), BF),
            vmem((4, 256, 1024), BF),
            vmem((512, 1024), BF),
            vmem((4, 8, 128, 256), BF),
            vmem((4, 8, 256), F32),
            vmem((16, 256, 256), BF),
            vmem((16, 1024, 256), BF),
            vmem((16, 1024, 256), BF),
            vmem((1024, 256), F32),
            vmem((4, 8, 128), F32),
            vmem((16, 8, 128), F32),
            vmem((8, 8, 128), F32),
            vmem((8, 128), F32),
            dma((6,)),
            dma((2, 4, 2)), dma((2, 4, 2)),
            dma((8,)), dma((8,)),
            dma((7,)), dma((7,)),
            dma((4, 4)), dma((4, 4)),
            dma((4,)), dma((4,)),
            dma((16,)), dma((16,)),
            dma((8,)), dma((8,)),
        ],
        compiler_params=pltpu.CompilerParams(
            collective_id=0, has_side_effects=True, vmem_limit_bytes=62 * 1024 * 1024),
        name="ladder",
    )(amplitudes, pmask, left_factor, right_t, qmask)
    return residual_in + ladder.reshape(residual_in.shape)


def solution(mesh):
    return jax.shard_map(
        local,
        mesh=mesh,
        in_specs=(
            P("occ", "vir", None),
            P("occ", "vir", None),
            P(None, "vir", "aux"),
            P("vir", "aux"),
            P(("occ", "vir"), None, "aux"),
            P(None, "aux"),
            P("occ", None, None),
        ),
        out_specs=P("occ", None, None),
        check_vma=False,
    )
```

time: 146 us -> 58.8 us (0.40)
  Pallas kernels: 0 us -> 52.7 us
  waiting for transfers between devices: 37.9 us -> 0 us
  blocking collectives: 30.7 us -> 0 us
  local copies, waits for them, and re-layouts: 32 us -> 4.47 us
  matrix products: 22.4 us -> 0 us
  starting transfers between devices: 15.6 us -> 0 us
  other arithmetic: 6.41 us -> 1.33 us
    pallas_call x0 -> x1, Pallas kernels: none -> 52.7 us  [local(): pl.pallas_call(kernel, out_shape=jax.ShapeDtypeStruct((8, 128), F32), in_...]
    all_to_all x2 -> x0, waiting for transfers between devices: 37.9 us -> none  [the longest x1 19.1 us: from_everyone(): return lax.all_to_all(copies, axis, split_axis=0, concat_axis=0, tiled=True)]
    all_to_all x2 -> x0, blocking collectives: 30.7 us -> none  [the longest x1 17.4 us: from_everyone(): return lax.all_to_all(copies, axis, split_axis=0, concat_axis=0, tiled=True)]
    dot_general x3 -> x0, matrix products: 22.4 us -> none  [the longest x1 13.2 us: local(): jnp.dot(tau_wide, couple_flat, precision=lax.Precision.HIGHEST, preferred...]
    all_to_all x2 -> x0, starting transfers between devices: 15.6 us -> none  [the longest x1 8.24 us: local(): lax.all_to_all(tau, 'occ', split_axis=2, concat_axis=0, tiled=True)]
    unnamed x12 -> x6, local copies, waits for them, and re-layouts: 17.3 us -> 3.03 us
    transpose x1 -> x0, local copies, waits for them, and re-layouts: 8.93 us -> none  [local(): jnp.einsum('acq,dbq->cdba', left, right_near, preferred_element_type=jnp....]
    all_to_all x3 -> x0, local copies, waits for them, and re-layouts: 3.83 us -> none  [the longest x1 3.25 us: local(): lax.all_to_all(tau, 'occ', split_axis=2, concat_axis=0, tiled=True)]
  transfers between devices with their start and end apart: 2 -> 0, of which waited for: 2 -> 0; matrix products, arithmetic and copies ran while one was open for 26% -> 0% of each run, Pallas kernels for 0% -> 0%
where the time goes in v1:
time: 58.8 us; the launch traced here: 58.5 us
  Pallas kernels  52.7 us (90%)
  local copies, waits for them, and re-layouts  4.47 us (8%)
  other arithmetic  1.33 us (2%)
    pallas_call x1, Pallas kernels, local(): pl.pallas_call(kernel, out_shape=jax.ShapeDtypeStruct((8, 128), F32), in_...  52.7 us
    unnamed x6, local copies, waits for them, and re-layouts  3.03 us

profile of v1, /device:TPU:1, one launch (start us, length us, event | category | flops | bytes accessed | tf_op | source)
XLA Modules:
  0.0 58.5 jit_solution(17592976699410936458)
XLA Ops:
  0.0 0.0 copy-start
  0.0 0.7 %multiply_convert_fusion = f32[2,8]{1,0:T(2,128)S(1)} fusion(s32[8,8]{1,0:T(8,128)} %param.12, s32[]{:T(128)S(6)} %select_n.9, s32[8]{0:T(128)} %bitcast.17), kind=kLoop, calls=%fused_computation.4 | loop fusion | flops 32 | bytes 164 | tf_op jit(solution)/shard_map/convert_element_type | solution.py:286
  0.7 0.8 %copy.8 = s32[8,1,8]{0,2,1:T(8,128)S(1)} copy(s32[8,1,8]{2,1,0:T(1,128)} %param.8) | data formatting | bytes 512 | tf_op args[1]
  1.5 0.1 broadcast_bitcast_fusion.1
  1.5 0.6 %copy.14 = f32[1,2,8,128]{3,1,2,0:T(2,128)} copy(f32[1,2,8,128]{3,2,1,0:T(8,128)S(1)} %broadcast_bitcast_fusion.1) | data formatting | bytes 16384
  2.2 0.7 %broadcast_bitcast_fusion.pmask = f32[4,8,256]{2,1,0:T(8,128)} fusion(f32[4,8,2]{1,2,0:T(2,128)S(1)} %bitcast.16), kind=kLoop, calls=%fused_computation.1 | loop fusion | bytes 33024 | tf_op jit(solution)/shard_map/reshape | solution.py:283
  2.8 1.6 %copy.13 = bf16[16,4,1024]{2,0,1:T(8,128)(2,1)} copy(bf16[16,4,1024]{2,1,0:T(4,128)(2,1)} %param.11) | data formatting | bytes 262144 | tf_op args[4]
  4.4 52.7 %ladder.1 = f32[8,128]{1,0:T(8,128)} custom-call(bf16[8,128,1024]{2,1,0:T(8,128)(2,1)} %amp.1, f32[4,8,256]{2,1,0:T(8,128)} %broadcast_bitcast_fusion.pmask, bf16[32,128,1024]{2,1,0:T(8,128)(2,1)} %left_h.1, bf16[4,16,1024]{2,1,0:T(8,128)(2,1)} %bitcast.14, f32[2,1024]{1,0:T(2,128)} %bitcast.15), custom_call_target="tpu_custom_call" | custom-call | tf_op jit(solution)/shard_map/ladder/pallas_call | solution.py:292
  57.2 0.8 %reshape.13 = f32[8,4,32]{2,1,0:T(4,128)S(1)} reshape(f32[8,128]{1,0:T(8,128)} %ladder.1) | data formatting | bytes 8192 | tf_op jit(solution)/shard_map/reshape | solution.py:324
  57.9 0.0 copy-done
  57.9 0.6 %add.8 = f32[8,4,32]{2,1,0:T(4,128)} add(f32[8,4,32]{2,1,0:T(4,128)S(1)} %copy-done, f32[8,4,32]{2,1,0:T(4,128)S(1)} %reshape.13) | non-fusion elementwise | flops 1024 | bytes 12288 | tf_op jit(solution)/shard_map/add | solution.py:324
  (1 shorter events, 0.0 us)
Async XLA Ops:
  0.0 57.9 %copy-start = (f32[8,4,32]{2,1,0:T(4,128)S(1)}, f32[8,4,32]{2,1,0:T(4,128)}, u32[]{:S(2)}) copy-start(f32[8,4,32]{2,1,0:T(4,128)} %param.13) | copy-start | bytes 12292

commit v2 on v1

v2 whole, which is shorter than its diff:
```python
import jax
import jax.numpy as jnp
from jax import lax
from jax.experimental import pallas as pl
from jax.experimental.pallas import tpu as pltpu
from jax.sharding import PartitionSpec as P

NX, NY, NZ = 4, 4, 8
BF, F32 = jnp.bfloat16, jnp.float32
MESH = pl.DeviceIdType.MESH
NT = (((1,), (1,)), ((), ()))


def mod(value, n):
    return lax.rem(value, n)


def device(x, y, z, core):
    return {"occ": 2 * x + lax.div(z, 4), "vir": 2 * mod(z, 4) + core, "aux": y}


def kernel(
    amp, pmask_h, left_h, lmask_h, right_h, rmask_h, out_ref,
    left, raw, rows, rside, tau0, tau1, tau2, tau3, pmask_v, lmask_v, rmask_v, qm, pmx, pm, tw, parts,
    grid_acc, part, got_xy, got_z, mine_z,
    local_sem, ring_send, ring_recv, pair_send, pair_recv,
    tx_send, tx_recv, ty_send, ty_recv, pm_send, pm_recv,
    xy_send, xy_recv, z_send, z_recv,
):
    occ, vir, y = lax.axis_index("occ"), lax.axis_index("vir"), lax.axis_index("aux")
    x, z, core = lax.div(occ, 2), mod(occ, 2) * 4 + lax.div(vir, 2), mod(vir, 2)
    here = pl.multiple_of(core * 16, 16)
    mine = pl.ds(pl.multiple_of(x * 256, 256), 256)

    tau = (tau0, tau1, tau2, tau3)

    own_right = pltpu.make_async_copy(right_h, raw, local_sem.at[4])
    own_tau = pltpu.make_async_copy(amp.at[:, :, mine], tau0, local_sem.at[5])
    small = [
        pltpu.make_async_copy(pmask_h, pmask_v, local_sem.at[6]),
        pltpu.make_async_copy(lmask_h, lmask_v, local_sem.at[7]),
        pltpu.make_async_copy(rmask_h, rmask_v, local_sem.at[8]),
    ]
    loads = [
        pltpu.make_async_copy(
            left_h.at[pl.ds(k * 8, 8)], left.at[pl.ds(k * 8, 8)], local_sem.at[k])
        for k in range(4)
    ]
    own_right.start()
    for copy in small:
        copy.start()
    for copy in loads:
        copy.start()
    own_tau.start()

    barrier = pltpu.get_barrier_semaphore()
    others = [device(mod(x + dx, NX), mod(y + dy, NY), z, core)
              for dx in range(NX) for dy in range(NY) if dx or dy]
    others += [device(x, y, mod(z + dz, NZ), core) for dz in (1, NZ - 1)]
    others += [{"occ": occ, "vir": mod(vir + dv, 8), "aux": y} for dv in range(1, 8)]
    for other in others:
        pl.semaphore_signal(barrier, inc=1, device_id=other, device_id_type=MESH)

    own_right.wait()
    wide = raw[...].astype(F32)
    for b in range(4):
        rows[b, pl.ds(32 + here, 16), :] = wide[:, b, :].astype(BF)
    for copy in small:
        copy.wait()
    tiles = (rmask_v[...] * lmask_v[...]).astype(F32)
    for q in range(8):
        qm[:, q * 128: q * 128 + 128] = jnp.broadcast_to(tiles[:, q: q + 1], (8, 128))
    ptile = pmask_v[...].reshape(8, 8).astype(F32)
    for t in range(8):
        pmx[t // 2, :, (t % 2) * 128: (t % 2) * 128 + 128] = jnp.broadcast_to(
            ptile[:, t: t + 1], (8, 128))
    pl.semaphore_wait(barrier, len(others))

    sent = []

    def go(copy):
        copy.start()
        sent.append(copy)

    def ring(way, step, b):
        src_i, dst_i = ((1 - step) % 8, (-step) % 8) if way == 0 else (1 + step, step + 2)
        to = mod(z + 1, NZ) if way == 0 else mod(z + NZ - 1, NZ)
        return pltpu.make_async_remote_copy(
            src_ref=rows.at[b, pl.ds(src_i * 32 + here, 16), :],
            dst_ref=rows.at[b, pl.ds(dst_i * 32 + here, 16), :],
            send_sem=ring_send.at[way, step, b], recv_sem=ring_recv.at[way, step, b],
            device_id=device(x, y, to, core), device_id_type=MESH)

    def pair(i):
        return pltpu.make_async_remote_copy(
            src_ref=rows.at[:, pl.ds(i * 32 + here, 16), :],
            dst_ref=rows.at[:, pl.ds(i * 32 + here, 16), :],
            send_sem=pair_send.at[i], recv_sem=pair_recv.at[i],
            device_id=device(x, y, z, 1 - core), device_id_type=MESH)

    def tau_x(dx, first, size):
        to = mod(x + dx, NX)
        return pltpu.make_async_remote_copy(
            src_ref=amp.at[pl.ds(first, size), :, pl.ds(pl.multiple_of(to * 256, 256), 256)],
            dst_ref=tau[(-dx) % 4].at[pl.ds(first, size)],
            send_sem=tx_send.at[dx], recv_sem=tx_recv.at[dx],
            device_id=device(to, y, z, core), device_id_type=MESH)

    def tau_y(dy):
        return pltpu.make_async_remote_copy(
            src_ref=tau2.at[pl.ds(2 * y, 2)], dst_ref=tau2.at[pl.ds(2 * y, 2)],
            send_sem=ty_send.at[dy], recv_sem=ty_recv.at[dy],
            device_id=device(x, mod(y + dy, NY), z, core), device_id_type=MESH)

    def mask_x(dx):
        to = mod(x + dx, NX)
        return pltpu.make_async_remote_copy(
            src_ref=pmx.at[to], dst_ref=pm.at[(-dx) % 4],
            send_sem=pm_send.at[dx], recv_sem=pm_recv.at[dx],
            device_id=device(to, y, z, core), device_id_type=MESH)

    x_copies = {1: tau_x(1, 0, 8), 2: tau_x(2, 2 * y, 2), 3: tau_x(3, 0, 8)}
    y_copies = {dy: tau_y(dy) for dy in (1, 2, 3)}
    masks = {dx: mask_x(dx) for dx in (1, 2, 3)}

    firsts = [[ring(way, 0, b) for way in (0, 1)] for b in range(4)]
    for b in range(4):
        for copy in firsts[b]:
            go(copy)
        if b == 0:
            go(pair(1))

    def arrived(way, step, b):
        ring(way, step, b).wait_recv()
        if step < 2 or (step == 2 and (b < 2) == (way == 0)):
            go(ring(way, step + 1, b))

    def stage(step, b):
        for way in (0, 1):
            if step < 3 or (b < 2) == (way == 0):
                arrived(way, step, b)

    def across(*chips):
        for i in chips:
            go(pair(i))

    def turn(slot):
        shift = mod(9 - z, 8) * 32

        def two(step, _):
            parts = []
            for k in range(2):
                p = step * 2 + k
                mask = (pmx[x, pl.ds(p, 1), :] if slot == 0 else pm[slot, pl.ds(p, 1), :])
                parts.append(pltpu.roll(tau[slot][p].astype(F32) * mask, shift, 1))
            first = pl.multiple_of(slot * 64 + step * 16, 16)
            for odd in range(2):
                if odd:
                    parts = [jnp.concatenate(
                        [pltpu.roll(v[:, h * 128: h * 128 + 128], 64, 1) for h in range(2)],
                        axis=1) for v in parts]
                for g in range(16):
                    both = jnp.concatenate([v[g * 8: g * 8 + 8, :] for v in parts], axis=0)
                    tw[odd, g, pl.ds(first, 16), :] = both.astype(BF)
            return 0

        lax.fori_loop(0, 4, two, 0)

    CHUNKS = {0: (0, 0, 0), 1: (2, 0, 1), 2: (6, 1, 1), 3: (4, 1, 0)}

    def gather(m):
        first, h, place = CHUNKS[m]
        for i in (first, first + 1):
            pair(i).wait_recv()
        for i in (first, first + 1):
            row = qm[pl.ds(2 * x + lax.div(mod(z + i + 7, NZ), 4), 1), :].astype(BF)
            for b in range(4):
                at = (b ^ place) * 64 + (i - first) * 32
                rside[at: at + 32, :] = rows[b, i * 32: i * 32 + 32, :] * row

    def couple(m, block):
        first, h, place = CHUNKS[m]
        lhs = left[pl.ds(block * 8, 8)].reshape(8 * 128, 1024)
        prod = lax.dot_general(lhs, rside[...], NT, preferred_element_type=F32)
        for g in range(16):
            blk = jnp.concatenate(
                [prod[a * 128 + g * 8: a * 128 + g * 8 + 8, :] for a in range(8)], axis=0)
            hi = blk.astype(BF)
            lo = (blk - hi.astype(F32)).astype(BF)
            for at in range(4):
                b = at ^ place
                lane = h * 128 + (at % 2) * 64
                for low, value in ((0, hi), (512, lo)):
                    top = pl.multiple_of(low + (b // 2) * 256 + block * 64, 64)
                    parts[g, b % 2, pl.ds(top, 64), lane: lane + 64] = (
                        value[:, at * 64: at * 64 + 64])

    def chunk(m):
        gather(m)
        lax.fori_loop(0, 4, lambda k, c: couple(m, k) or c, 0)

    def passed(step):
        for b in range(4):
            stage(step, b)

    for copy in loads:
        copy.wait()
    passed(0)
    across(0, 2)
    for dx in (2, 1, 3):
        go(x_copies[dx])
    for copy in masks.values():
        go(copy)
    chunk(0)
    x_copies[2].wait_recv()
    for dy in (2, 1, 3):
        go(y_copies[dy])
    passed(1)
    across(3, 7)
    own_tau.wait()
    turn(0)
    chunk(1)
    passed(2)
    across(4, 6)
    for dx in (1, 2, 3):
        masks[dx].wait_recv()
    for dy in (1, 2, 3):
        y_copies[dy].wait_recv()
    turn(2)
    chunk(2)
    passed(3)
    across(5)
    x_copies[3].wait_recv()
    turn(1)
    x_copies[1].wait_recv()
    turn(3)
    chunk(3)

    grid_acc[...] = jnp.zeros_like(grid_acc)

    def contract(step, _):
        for odd in range(2):
            total = jnp.zeros((1024, 256), F32)
            for k in range(4):
                g = step * 4 + k
                total = total + lax.dot_general(
                    parts[g, odd], tw[odd, g], NT, preferred_element_type=F32)
            grid_acc[odd * 512: odd * 512 + 512, :] += total[:512] + total[512:]
        return 0

    lax.fori_loop(0, 4, contract, 0)

    acc = grid_acc[...].reshape(128, 8, 256)
    same = (lax.broadcasted_iota(jnp.int32, (128, 8, 256), 2) % 8
            == lax.broadcasted_iota(jnp.int32, (128, 8, 256), 1))
    diag = jnp.where(same, acc, 0.0).sum(axis=1)
    pick = (lax.broadcasted_iota(jnp.int32, (32, 256), 1) // 8
            == lax.broadcasted_iota(jnp.int32, (32, 256), 0)).astype(F32).astype(BF)
    ladder = jnp.zeros((32, 128), F32)
    rest = diag
    for _ in range(3):
        top = rest.astype(BF)
        rest = rest - top.astype(F32)
        ladder = ladder + lax.dot_general(pick, top, NT, preferred_element_type=F32)
    part[...] = ladder.reshape(4, 8, 128)

    index = x * 4 + y
    got_xy[index] = part[0]

    def to_xy(dx, dy):
        return pltpu.make_async_remote_copy(
            src_ref=part.at[dx], dst_ref=got_xy.at[index],
            send_sem=xy_send.at[dx * 4 + dy], recv_sem=xy_recv.at[dx * 4 + dy],
            device_id=device(mod(x + dx, NX), mod(y + dy, NY), z, core), device_id_type=MESH)

    total = part[0]
    pairs = [(dx, dy) for dx in range(4) for dy in range(4) if dx or dy]
    xy = [to_xy(dx, dy) for dx, dy in sorted(pairs, key=lambda d: -(d[0] == 2) - (d[1] == 2))]
    for copy in xy:
        go(copy)
    for copy in xy:
        copy.wait_recv()
    total = got_xy[0]
    for k in range(1, 16):
        total = total + got_xy[k]
    mine_z[...] = total
    got_z[vir] = total

    def to_z(dv):
        return pltpu.make_async_remote_copy(
            src_ref=mine_z, dst_ref=got_z.at[vir],
            send_sem=z_send.at[dv], recv_sem=z_recv.at[dv],
            device_id={"occ": occ, "vir": mod(vir + dv, 8), "aux": y}, device_id_type=MESH)

    zs = [to_z(dv) for dv in range(1, 8)]
    for copy in zs:
        go(copy)
    for copy in zs:
        copy.wait_recv()
    total = got_z[0]
    for k in range(1, 8):
        total = total + got_z[k]
    for at, b in enumerate((0, 2, 1, 3)):
        out_ref[pl.ds(b, 8, stride=4), :] = total[:, at * 32: at * 32 + 32]
    for copy in sent:
        copy.wait_send()


def local(amplitudes, pair_mask, left_factor, left_mask, right_factor, right_mask, residual_in):
    dma = pltpu.SemaphoreType.DMA
    vmem = pltpu.VMEM
    ladder = pl.pallas_call(
        kernel,
        out_shape=jax.ShapeDtypeStruct((32, 32), F32),
        in_specs=[pl.BlockSpec(memory_space=pl.ANY)] * 6,
        out_specs=pl.BlockSpec(memory_space=pltpu.VMEM),
        scratch_shapes=[
            vmem((32, 128, 1024), BF),
            vmem((16, 4, 1024), BF),
            vmem((4, 256, 1024), BF),
            vmem((256, 1024), BF),
            vmem((8, 128, 256), BF), vmem((8, 128, 256), BF),
            vmem((8, 128, 256), BF), vmem((8, 128, 256), BF),
            vmem((8, 1, 8), jnp.int32),
            vmem((1, 8), jnp.int32),
            vmem((8, 8), jnp.int32),
            vmem((8, 1024), F32),
            vmem((4, 8, 256), F32),
            vmem((4, 8, 256), F32),
            vmem((2, 16, 256, 256), BF),
            vmem((16, 2, 1024, 256), BF),
            vmem((1024, 256), F32),
            vmem((4, 8, 128), F32),
            vmem((16, 8, 128), F32),
            vmem((8, 8, 128), F32),
            vmem((8, 128), F32),
            dma((9,)),
            dma((2, 4, 4)), dma((2, 4, 4)),
            dma((8,)), dma((8,)),
            dma((4,)), dma((4,)),
            dma((4,)), dma((4,)),
            dma((4,)), dma((4,)),
            dma((16,)), dma((16,)),
            dma((8,)), dma((8,)),
        ],
        compiler_params=pltpu.CompilerParams(
            collective_id=0, has_side_effects=True, vmem_limit_bytes=62 * 1024 * 1024),
        name="ladder",
    )(amplitudes, pair_mask, left_factor, left_mask, right_factor, right_mask)
    return residual_in + ladder.reshape(residual_in.shape)


def solution(mesh):
    return jax.shard_map(
        local,
        mesh=mesh,
        in_specs=(
            P("occ", "vir", None),
            P("occ", "vir", None),
            P(None, "vir", "aux"),
            P("vir", "aux"),
            P(("occ", "vir"), None, "aux"),
            P(None, "aux"),
            P("occ", None, None),
        ),
        out_specs=P("occ", None, None),
        check_vma=False,
    )
```

time: 58.8 us -> 60.1 us (1.022)
  Pallas kernels: 52.7 us -> 58.5 us
  local copies, waits for them, and re-layouts: 4.47 us -> 0.01 us
    pallas_call x1, Pallas kernels: 52.7 us -> 58.5 us  [local(): pl.pallas_call(kernel, out_shape=jax.ShapeDtypeStruct((32, 32), F32), in_...]
    unnamed x6 -> x2, local copies, waits for them, and re-layouts: 3.03 us -> 0.01 us
    reshape x2 -> x0, local copies, waits for them, and re-layouts: 1.44 us -> none  [the longest x1 0.76 us: local(): return residual_in + ladder.reshape(residual_in.shape)]
    add x1, other arithmetic: 0.61 us -> 1.33 us  [local(): return residual_in + ladder.reshape(residual_in.shape)]
    convert_element_type x2 -> x0, other arithmetic: 0.71 us -> none  [the longest x1 0.71 us: local(): qmask = jnp.repeat(tiles.astype(F32), TILE, axis=1)]
where the time goes in v2:
time: 60.1 us; the launch traced here: 59.9 us
  Pallas kernels  58.5 us (97%)
  other arithmetic  1.33 us (2%)
    pallas_call x1, Pallas kernels, local(): pl.pallas_call(kernel, out_shape=jax.ShapeDtypeStruct((32, 32), F32), in_...  58.5 us
    add x1, other arithmetic, local(): return residual_in + ladder.reshape(residual_in.shape)  1.33 us

profile of v2, /device:TPU:1, one launch (start us, length us, event | category | flops | bytes accessed | tf_op | source)
XLA Modules:
  0.0 59.9 jit_solution(10545828222906335377)
XLA Ops:
  0.0 0.0 copy-start
  0.0 58.5 %ladder.1 = f32[32,32]{1,0:T(8,128)} custom-call(bf16[8,128,1024]{2,1,0:T(8,128)(2,1)} %amp.1, s32[8,1,8]{2,1,0:T(1,128)} %pmask_h.1, bf16[32,128,1024]{2,1,0:T(8,128)(2,1)} %left_h.1, s32[1,8]{1,0:T(1,128)} %lmask_h.1, bf16[16,4,1024]{2,1,0:T(4,128)(2,1)} %right_h.1, s32[8,8]{1,0:T(8,128)} %rmask_h.1), custom_call_target="tpu_custom_call" | custom-call | tf_op jit(solution)/shard_map/ladder/pallas_call | solution.py:312
  58.5 0.0 copy-done
  58.5 1.3 %add.3 = f32[8,4,32]{2,1,0:T(4,128)} add(f32[8,4,32]{2,1,0:T(4,128)S(1)} %copy-done, f32[8,4,32]{2,1,0:T(4,128)} %bitcast.1) | non-fusion elementwise | flops 1024 | bytes 12288 | tf_op jit(solution)/shard_map/add | solution.py:350
Async XLA Ops:
  0.0 58.5 %copy-start = (f32[8,4,32]{2,1,0:T(4,128)S(1)}, f32[8,4,32]{2,1,0:T(4,128)}, u32[]{:S(2)}) copy-start(f32[8,4,32]{2,1,0:T(4,128)} %param.13) | copy-start | bytes 12292

commit v3 on v2

--- a/solution.py
+++ b/solution.py
@@ -78,9 +78,9 @@
 
     sent = []
 
-    def go(copy):
-        copy.start()
-        sent.append(copy)
+    def go(make, *args):
+        make(*args).start()
+        sent.append((make, args))
 
     def ring(way, step, b):
         src_i, dst_i = ((1 - step) % 8, (-step) % 8) if way == 0 else (1 + step, step + 2)
@@ -119,30 +119,30 @@
             send_sem=pm_send.at[dx], recv_sem=pm_recv.at[dx],
             device_id=device(to, y, z, core), device_id_type=MESH)
 
-    x_copies = {1: tau_x(1, 0, 8), 2: tau_x(2, 2 * y, 2), 3: tau_x(3, 0, 8)}
-    y_copies = {dy: tau_y(dy) for dy in (1, 2, 3)}
-    masks = {dx: mask_x(dx) for dx in (1, 2, 3)}
-
-    firsts = [[ring(way, 0, b) for way in (0, 1)] for b in range(4)]
+    SPAN = {1: (0, 8), 2: (2 * y, 2), 3: (0, 8)}
     for b in range(4):
-        for copy in firsts[b]:
-            go(copy)
+        for way in (0, 1):
+            go(ring, way, 0, b)
         if b == 0:
-            go(pair(1))
+            go(pair, 1)
+    for dx in (1, 2, 3):
+        go(mask_x, dx)
+    go(tau_x, 2, *SPAN[2])
 
     def arrived(way, step, b):
         ring(way, step, b).wait_recv()
         if step < 2 or (step == 2 and (b < 2) == (way == 0)):
-            go(ring(way, step + 1, b))
-
-    def stage(step, b):
-        for way in (0, 1):
-            if step < 3 or (b < 2) == (way == 0):
-                arrived(way, step, b)
+            go(ring, way, step + 1, b)
+
+    def passed(step):
+        for b in range(4):
+            for way in (0, 1):
+                if step < 3 or (b < 2) == (way == 0):
+                    arrived(way, step, b)
 
     def across(*chips):
         for i in chips:
-            go(pair(i))
+            go(pair, i)
 
     def turn(slot):
         shift = mod(9 - z, 8) * 32
@@ -166,20 +166,19 @@
 
         lax.fori_loop(0, 4, two, 0)
 
-    CHUNKS = {0: (0, 0, 0), 1: (2, 0, 1), 2: (6, 1, 1), 3: (4, 1, 0)}
-
-    def gather(m):
-        first, h, place = CHUNKS[m]
-        for i in (first, first + 1):
-            pair(i).wait_recv()
-        for i in (first, first + 1):
+    def gather(m, first, place):
+        for k in range(2):
+            pair(first + k).wait_recv()
+        for k in range(2):
+            i = first + k
             row = qm[pl.ds(2 * x + lax.div(mod(z + i + 7, NZ), 4), 1), :].astype(BF)
-            for b in range(4):
-                at = (b ^ place) * 64 + (i - first) * 32
-                rside[at: at + 32, :] = rows[b, i * 32: i * 32 + 32, :] * row
-
-    def couple(m, block):
-        first, h, place = CHUNKS[m]
+            from_row = pl.multiple_of(i * 32, 32)
+            for at in range(4):
+                b = (at // 2) * 2 + mod(at + place, 2)
+                rside[at * 64 + k * 32: at * 64 + k * 32 + 32, :] = (
+                    rows[b, pl.ds(from_row, 32), :] * row)
+
+    def couple(h, place, block):
         lhs = left[pl.ds(block * 8, 8)].reshape(8 * 128, 1024)
         prod = lax.dot_general(lhs, rside[...], NT, preferred_element_type=F32)
         for g in range(16):
@@ -188,53 +187,63 @@
             hi = blk.astype(BF)
             lo = (blk - hi.astype(F32)).astype(BF)
             for at in range(4):
-                b = at ^ place
-                lane = h * 128 + (at % 2) * 64
+                lane = (at % 2) * 64
                 for low, value in ((0, hi), (512, lo)):
-                    top = pl.multiple_of(low + (b // 2) * 256 + block * 64, 64)
-                    parts[g, b % 2, pl.ds(top, 64), lane: lane + 64] = (
+                    top = pl.multiple_of(low + (at // 2) * 256 + block * 64, 64)
+                    parts[h, g, mod(at + place, 2), pl.ds(top, 64), lane: lane + 64] = (
                         value[:, at * 64: at * 64 + 64])
 
-    def chunk(m):
-        gather(m)
-        lax.fori_loop(0, 4, lambda k, c: couple(m, k) or c, 0)
-
-    def passed(step):
-        for b in range(4):
-            stage(step, b)
-
+    own_tau.wait()
+    turn(0)
     for copy in loads:
         copy.wait()
     passed(0)
     across(0, 2)
-    for dx in (2, 1, 3):
-        go(x_copies[dx])
-    for copy in masks.values():
-        go(copy)
-    chunk(0)
-    x_copies[2].wait_recv()
+    go(tau_x, 1, *SPAN[1])
+    go(tau_x, 3, *SPAN[3])
+    tau_x(2, *SPAN[2]).wait_recv()
     for dy in (2, 1, 3):
-        go(y_copies[dy])
-    passed(1)
-    across(3, 7)
-    own_tau.wait()
-    turn(0)
-    chunk(1)
-    passed(2)
-    across(4, 6)
-    for dx in (1, 2, 3):
-        masks[dx].wait_recv()
-    for dy in (1, 2, 3):
-        y_copies[dy].wait_recv()
-    turn(2)
-    chunk(2)
-    passed(3)
-    across(5)
-    x_copies[3].wait_recv()
-    turn(1)
-    x_copies[1].wait_recv()
-    turn(3)
-    chunk(3)
+        go(tau_y, dy)
+
+    def chunk(m, _):
+        h = lax.div(m, 2)
+        place = mod(h + m, 2)
+        gather(m, 2 * m + h * (10 - 4 * m), place)
+
+        def two(k, _):
+            couple(h, place, 2 * k)
+            couple(h, place, 2 * k + 1)
+            return 0
+
+        lax.fori_loop(0, 2, two, 0)
+
+        @pl.when(m == 0)
+        def _():
+            passed(1)
+            across(3, 7)
+
+        @pl.when(m == 1)
+        def _():
+            passed(2)
+            across(4, 6)
+            for dx in (1, 2, 3):
+                mask_x(dx).wait_recv()
+            for dy in (1, 2, 3):
+                tau_y(dy).wait_recv()
+            turn(2)
+
+        @pl.when(m == 2)
+        def _():
+            passed(3)
+            across(5)
+            tau_x(3, *SPAN[3]).wait_recv()
+            turn(1)
+            tau_x(1, *SPAN[1]).wait_recv()
+            turn(3)
+
+        return 0
+
+    lax.fori_loop(0, 4, chunk, 0)
 
     grid_acc[...] = jnp.zeros_like(grid_acc)
 
@@ -243,8 +252,9 @@
             total = jnp.zeros((1024, 256), F32)
             for k in range(4):
                 g = step * 4 + k
+                both = jnp.concatenate([parts[0, g, odd], parts[1, g, odd]], axis=1)
                 total = total + lax.dot_general(
-                    parts[g, odd], tw[odd, g], NT, preferred_element_type=F32)
+                    both, tw[odd, g], NT, preferred_element_type=F32)
             grid_acc[odd * 512: odd * 512 + 512, :] += total[:512] + total[512:]
         return 0
 
@@ -275,11 +285,11 @@
 
     total = part[0]
     pairs = [(dx, dy) for dx in range(4) for dy in range(4) if dx or dy]
-    xy = [to_xy(dx, dy) for dx, dy in sorted(pairs, key=lambda d: -(d[0] == 2) - (d[1] == 2))]
-    for copy in xy:
-        go(copy)
-    for copy in xy:
-        copy.wait_recv()
+    pairs.sort(key=lambda d: -(d[0] == 2) - (d[1] == 2))
+    for dx, dy in pairs:
+        go(to_xy, dx, dy)
+    for dx, dy in pairs:
+        to_xy(dx, dy).wait_recv()
     total = got_xy[0]
     for k in range(1, 16):
         total = total + got_xy[k]
@@ -292,18 +302,17 @@
             send_sem=z_send.at[dv], recv_sem=z_recv.at[dv],
             device_id={"occ": occ, "vir": mod(vir + dv, 8), "aux": y}, device_id_type=MESH)
 
-    zs = [to_z(dv) for dv in range(1, 8)]
-    for copy in zs:
-        go(copy)
-    for copy in zs:
-        copy.wait_recv()
+    for dv in range(1, 8):
+        go(to_z, dv)
+    for dv in range(1, 8):
+        to_z(dv).wait_recv()
     total = got_z[0]
     for k in range(1, 8):
         total = total + got_z[k]
     for at, b in enumerate((0, 2, 1, 3)):
         out_ref[pl.ds(b, 8, stride=4), :] = total[:, at * 32: at * 32 + 32]
-    for copy in sent:
-        copy.wait_send()
+    for make, args in sent:
+        make(*args).wait_send()
 
 
 def local(amplitudes, pair_mask, left_factor, left_mask, right_factor, right_mask, residual_in):
@@ -328,7 +337,7 @@
             vmem((4, 8, 256), F32),
             vmem((4, 8, 256), F32),
             vmem((2, 16, 256, 256), BF),
-            vmem((16, 2, 1024, 256), BF),
+            vmem((2, 16, 2, 1024, 128), BF),
             vmem((1024, 256), F32),
             vmem((4, 8, 128), F32),
             vmem((16, 8, 128), F32),

time: 60.1 us -> 54.5 us (0.907)
  Pallas kernels: 58.5 us -> 53 us
    pallas_call x1, Pallas kernels: 58.5 us -> 53 us  [local(): pl.pallas_call(kernel, out_shape=jax.ShapeDtypeStruct((32, 32), F32), in_...]
where the time goes in v3:
time: 54.5 us; the launch traced here: 54.3 us
  Pallas kernels  53 us (97%)
  other arithmetic  1.33 us (2%)
    pallas_call x1, Pallas kernels, local(): pl.pallas_call(kernel, out_shape=jax.ShapeDtypeStruct((32, 32), F32), in_...  53 us
    add x1, other arithmetic, local(): return residual_in + ladder.reshape(residual_in.shape)  1.33 us

profile of v3, /device:TPU:1, one launch (start us, length us, event | category | flops | bytes accessed | tf_op | source)
XLA Modules:
  0.0 54.3 jit_solution(17446948015730320689)
XLA Ops:
  0.0 0.0 copy-start
  0.0 53.0 %ladder.1 = f32[32,32]{1,0:T(8,128)} custom-call(bf16[8,128,1024]{2,1,0:T(8,128)(2,1)} %amp.1, s32[8,1,8]{2,1,0:T(1,128)} %pmask_h.1, bf16[32,128,1024]{2,1,0:T(8,128)(2,1)} %left_h.1, s32[1,8]{1,0:T(1,128)} %lmask_h.1, bf16[16,4,1024]{2,1,0:T(4,128)(2,1)} %right_h.1, s32[8,8]{1,0:T(8,128)} %rmask_h.1), custom_call_target="tpu_custom_call" | custom-call | tf_op jit(solution)/shard_map/ladder/pallas_call | solution.py:321
  53.0 0.0 copy-done
  53.0 1.3 %add.3 = f32[8,4,32]{2,1,0:T(4,128)} add(f32[8,4,32]{2,1,0:T(4,128)S(1)} %copy-done, f32[8,4,32]{2,1,0:T(4,128)} %bitcast.1) | non-fusion elementwise | flops 1024 | bytes 12288 | tf_op jit(solution)/shard_map/add | solution.py:359
Async XLA Ops:
  0.0 53.0 %copy-start = (f32[8,4,32]{2,1,0:T(4,128)S(1)}, f32[8,4,32]{2,1,0:T(4,128)}, u32[]{:S(2)}) copy-start(f32[8,4,32]{2,1,0:T(4,128)} %param.13) | copy-start | bytes 12292

commit v4 on v3

--- a/solution.py
+++ b/solution.py
@@ -43,7 +43,8 @@
     ]
     loads = [
         pltpu.make_async_copy(
-            left_h.at[pl.ds(k * 8, 8)], left.at[pl.ds(k * 8, 8)], local_sem.at[k])
+            left_h.at[pl.ds(k * 8, 8)], left.at[pl.ds(k * 8, 8), :, pl.ds(0, 1024)],
+            local_sem.at[k])
         for k in range(4)
     ]
     own_right.start()
@@ -179,19 +180,22 @@
                     rows[b, pl.ds(from_row, 32), :] * row)
 
     def couple(h, place, block):
-        lhs = left[pl.ds(block * 8, 8)].reshape(8 * 128, 1024)
+        lhs = left[pl.ds(block * 8, 8), :, 0:1024].reshape(8 * 128, 1024)
         prod = lax.dot_general(lhs, rside[...], NT, preferred_element_type=F32)
-        for g in range(16):
-            blk = jnp.concatenate(
-                [prod[a * 128 + g * 8: a * 128 + g * 8 + 8, :] for a in range(8)], axis=0)
-            hi = blk.astype(BF)
-            lo = (blk - hi.astype(F32)).astype(BF)
-            for at in range(4):
-                lane = (at % 2) * 64
-                for low, value in ((0, hi), (512, lo)):
-                    top = pl.multiple_of(low + (at // 2) * 256 + block * 64, 64)
-                    parts[h, g, mod(at + place, 2), pl.ds(top, 64), lane: lane + 64] = (
-                        value[:, at * 64: at * 64 + 64])
+        for pair_a in range(4):
+            for g in range(16):
+                at_a = pair_a * 256 + g * 8
+                blk = jnp.concatenate(
+                    [prod[at_a: at_a + 8, :], prod[at_a + 128: at_a + 136, :]], axis=0)
+                hi = blk.astype(BF)
+                lo = (blk - hi.astype(F32)).astype(BF)
+                for at in range(4):
+                    lane = (at % 2) * 64
+                    for low, value in ((0, hi), (512, lo)):
+                        top = pl.multiple_of(
+                            low + (at // 2) * 256 + block * 64 + pair_a * 16, 16)
+                        parts[h, g, mod(at + place, 2), pl.ds(top, 16), lane: lane + 64] = (
+                            value[:, at * 64: at * 64 + 64])
 
     own_tau.wait()
     turn(0)
@@ -324,7 +328,7 @@
         in_specs=[pl.BlockSpec(memory_space=pl.ANY)] * 6,
         out_specs=pl.BlockSpec(memory_space=pltpu.VMEM),
         scratch_shapes=[
-            vmem((32, 128, 1024), BF),
+            vmem((32, 128, 1152), BF),
             vmem((16, 4, 1024), BF),
             vmem((4, 256, 1024), BF),
             vmem((256, 1024), BF),

time: 54.5 us -> 53 us (0.972)
  Pallas kernels: 53 us -> 51.5 us
    pallas_call x1, Pallas kernels: 53 us -> 51.5 us  [local(): pl.pallas_call(kernel, out_shape=jax.ShapeDtypeStruct((32, 32), F32), in_...]
where the time goes in v4:
time: 53 us; the launch traced here: 52.8 us
  Pallas kernels  51.5 us (97%)
  other arithmetic  1.33 us (3%)
    pallas_call x1, Pallas kernels, local(): pl.pallas_call(kernel, out_shape=jax.ShapeDtypeStruct((32, 32), F32), in_...  51.5 us
    add x1, other arithmetic, local(): return residual_in + ladder.reshape(residual_in.shape)  1.33 us

profile of v4, /device:TPU:1, one launch (start us, length us, event | category | flops | bytes accessed | tf_op | source)
XLA Modules:
  0.0 52.8 jit_solution(8978814650876307352)
XLA Ops:
  0.0 0.0 copy-start
  0.0 51.5 %ladder.1 = f32[32,32]{1,0:T(8,128)} custom-call(bf16[8,128,1024]{2,1,0:T(8,128)(2,1)} %amp.1, s32[8,1,8]{2,1,0:T(1,128)} %pmask_h.1, bf16[32,128,1024]{2,1,0:T(8,128)(2,1)} %left_h.1, s32[1,8]{1,0:T(1,128)} %lmask_h.1, bf16[16,4,1024]{2,1,0:T(4,128)(2,1)} %right_h.1, s32[8,8]{1,0:T(8,128)} %rmask_h.1), custom_call_target="tpu_custom_call" | custom-call | tf_op jit(solution)/shard_map/ladder/pallas_call | solution.py:325
  51.5 0.0 copy-done
  51.5 1.3 %add.3 = f32[8,4,32]{2,1,0:T(4,128)} add(f32[8,4,32]{2,1,0:T(4,128)S(1)} %copy-done, f32[8,4,32]{2,1,0:T(4,128)} %bitcast.1) | non-fusion elementwise | flops 1024 | bytes 12288 | tf_op jit(solution)/shard_map/add | solution.py:363
Async XLA Ops:
  0.0 51.5 %copy-start = (f32[8,4,32]{2,1,0:T(4,128)S(1)}, f32[8,4,32]{2,1,0:T(4,128)}, u32[]{:S(2)}) copy-start(f32[8,4,32]{2,1,0:T(4,128)} %param.13) | copy-start | bytes 12292
